TPU v7x, 512 devices: a whole 4x8x8 slice. The times are simulated.
512 devices in a mesh: dp: 128 (over z, y, core), mp: 4 (over x).
Axes of the slice: x: 4, y: 8, z: 8, core: 2. Of those that a mesh axis runs over, the one named last changes fastest.
Arguments:
- bag_lengths: int32 [16, 16384], P('mp', 'dp'), may hold values from 1 to 8
- owners: int32 [16, 16384, 8, 1], P('mp', 'dp'), may hold values from 0 to 127; in each aligned block of 1024 rows (0 to 1023, 1024 to 2047, ..., all dimensions but the last counted through in order) at most 16 rows name the same one
- row_slots: int32 [16, 16384, 8], P('mp', 'dp'), may hold values from 0 to 511
- admit_mask: int32 [16, 16384, 8], P('mp', 'dp'), may hold values 0 or 1
- expired: int32 [16, 65536], P('mp', 'dp'), may hold values 0 or 1
- embeddings: float32 [16, 65536, 128], P('mp', 'dp'), may hold values from -3 to 3
- accumulator: float32 [16, 65536], P('mp', 'dp'), may hold values from 0.001 to 0.01
- hidden_weight: bfloat16 [2048, 1024], P(None, 'mp'), may hold values from -0.125 to 0.125
- output_weight: float32 [1024], P('mp'), may hold values from -0.9 to 0.9
- labels: int32 [16384], P('dp'), may hold values 0 or 1
Outputs:
- new_table: float32 [16, 65536, 128], P('mp', 'dp')
- new_accum: float32 [16, 65536], P('mp', 'dp')
- weight_grad: bfloat16 [2048, 1024], P(None, 'mp')
- logits: float32 [16384], P('dp')
Inputs may be any that keep to these rules, and one draw needn't show every extreme that they name: Among the 128 x 8 lookups of one index of dp into one table (aligned blocks of owners' rows), at most 16 name the same owner; in some blocks one owner is named exactly 16 times.
All inputs are finite; a program needn't handle non-finite values. No bound on the sum of `admit_mask` or of `expired` or of `labels` on one device may be relied on, other than what follows from the above.
Results may differ from a plain program's by a relative error of at most 0.0085.
Values may be sent and summed in bfloat16 or wider, within the bound.
No kernel may reach another device: no remote copies, remote signals or barrier semaphores. Data moves between devices by JAX's collectives and lax.ppermute only.
A program may use at most 64 MiB of HBM per device.

v0:
```python
import functools

import jax
import jax.numpy as jnp
from jax import lax
from jax.experimental import pallas as pl
from jax.experimental.pallas import tpu as pltpu
from jax.sharding import Mesh
from jax.sharding import PartitionSpec as P

DP = ("dp_0", "dp_1", "dp_2")
FAR = ("dp_0", "dp_1")
NEAR = "dp_2"

LEARN_RATE = 0.05
ACC_RESET = 0.001
F32, BF16, I32 = jnp.float32, jnp.bfloat16, jnp.int32
NT = (((1,), (1,)), ((), ()))


def iota(shape, dim):
    return lax.broadcasted_iota(I32, shape, dim)


def dot(a, b, dims=(((1,), (0,)), ((), ()))):
    return lax.dot_general(a, b, dims, preferred_element_type=F32)


def flag(cond):
    return jnp.where(cond, 1.0, 0.0).astype(BF16)


def slots_kernel(len_ref, own_ref, slot_ref, adm_ref, req_ref, sample_ref, inv_ref):
    tabs, bag, toks = own_ref.shape
    groups, width = req_ref.shape
    cap = width // tabs
    square = (toks, toks)
    tri = jnp.concatenate(
        [flag(iota(square, 0) < iota(square, 1)), jnp.ones(square, BF16)], axis=1
    )
    rank_row = iota((cap, toks), 0).astype(F32)
    sample_no = (iota((1, toks), 1) + 1).astype(F32)
    name = iota((groups, toks), 0).astype(F32).astype(BF16)
    one, zero = jnp.ones((groups, toks), BF16), jnp.zeros((groups, toks), BF16)
    hot, counts = [], []
    for t in range(tabs):
        owner = own_ref[t].astype(F32)
        rows = [jnp.broadcast_to(owner[p : p + 1], (groups, toks)) for p in range(bag)]
        hot.append([jnp.where(name == row.astype(BF16), one, zero) for row in rows])
        counts.append(dot(jnp.concatenate(hot[t], axis=0), tri))
    for t in range(tabs):
        base = jnp.zeros((groups, toks), F32)
        live_count = jnp.zeros((1, toks), F32)
        values = []
        for p in range(bag):
            part = counts[t][p * groups : (p + 1) * groups]
            before = part[:, :toks] + base
            rank = jnp.sum(hot[t][p].astype(F32) * before, axis=0, keepdims=True)
            base = base + part[:, toks:]
            live = (p < len_ref[t : t + 1, :]) & (adm_ref[t, p : p + 1, :] == 1)
            live_count = live_count + jnp.where(live, 1.0, 0.0)
            slot = slot_ref[t, p : p + 1, :]
            here = rank_row == rank
            values.append(
                jnp.concatenate(
                    [
                        jnp.where(here, (slot >> 4).astype(F32), 0.0),
                        jnp.where(here, (slot & 15).astype(F32), 0.0),
                        jnp.where(here & live, sample_no, 0.0),
                    ],
                    axis=0,
                ).astype(BF16)
            )
        found = dot(jnp.concatenate(hot[t], axis=1), jnp.concatenate(values, axis=1), NT)
        cols = slice(t * cap, (t + 1) * cap)
        req_ref[:, cols] = (16.0 * found[:, :cap] + found[:, cap : 2 * cap]).astype(I32)
        sample_ref[:, cols] = found[:, 2 * cap :]
        inv = 1.0 / jnp.maximum(live_count, 1.0)
        column = jnp.sum(
            jnp.where(iota(square, 0) == iota(square, 1), inv, 0.0), axis=1, keepdims=True
        )
        inv_ref[t] = jnp.broadcast_to(column, square)


def own_lines(table, slots):
    groups, lanes = table.shape
    cap = slots // groups
    mine = iota((cap, lanes), 1) % cap == iota((cap, lanes), 0)
    return jnp.concatenate(
        [
            jnp.where(mine, jnp.broadcast_to(table[o : o + 1], (cap, lanes)), 0.0)
            for o in range(groups)
        ],
        axis=0,
    ).astype(BF16)


def of_table(shape, lane_dim, t, kind, width, cap):
    lane = iota(shape, lane_dim)
    return flag((lane // width == kind) & (lane % width // cap == t))


def samples_kernel(sample_ref, pick_ref, row_ref):
    tabs, slots, toks = pick_ref.shape
    width = sample_ref.shape[1]
    cap = width // tabs
    own = own_lines(sample_ref[...], slots)
    wanted = (iota((slots, toks), 1) + 1).astype(F32)
    for t in range(tabs):
        mine = of_table((width, toks), 0, t, 0, width, cap)
        pick_ref[t] = flag(dot(own, mine) == wanted)
        row = dot(of_table((8, width), 1, t, 0, width, cap), own, NT)
        row_ref[t : t + 1, :] = row[0:1]


def labels_kernel(label_ref, out_ref):
    dims = out_ref.shape
    row = label_ref[...].astype(F32)
    column = jnp.sum(
        jnp.where(iota(dims, 0) == iota(dims, 1), row, 0.0), axis=1, keepdims=True
    )
    out_ref[...] = jnp.broadcast_to(column, dims)


def halves_of(arrived, block_rows):
    shift = block_rows.bit_length() - 1
    return jnp.concatenate(
        [(arrived >> shift).astype(F32), (arrived & (block_rows - 1)).astype(F32)], axis=1
    )


def fetch_kernel(
    arrived_ref, expired_ref, emb_ref, out_ref,
    gone_ref, held_ref, table_ref, sent_ref, in_sem, out_sem,
):
    groups, width = arrived_ref.shape
    tabs, rows, emb = emb_ref.shape
    cap = width // tabs
    half = rows // 2
    loads = [pltpu.make_async_copy(expired_ref, gone_ref, in_sem.at[tabs])] + [
        pltpu.make_async_copy(emb_ref.at[t], held_ref.at[t], in_sem.at[t]) for t in range(tabs)
    ]
    for load in loads:
        load.start()
    arrived = arrived_ref[...]
    place = (arrived & (half - 1)) + 1
    signed = jnp.where(arrived < half, place, -place).astype(F32).T.astype(BF16)
    parts = out_sem.shape[0]
    part = groups // parts
    lane = (iota((cap, emb), 1) + 1).astype(F32)
    names = lane.astype(BF16), (lane + emb).astype(BF16)
    one, zero = jnp.ones((cap, emb), BF16), jnp.zeros((cap, emb), BF16)
    stores = []
    for c in range(parts):
        mine = slice(c * part, (c + 1) * part)
        for t in range(tabs):
            if c == 0:
                if t == 0:
                    loads[0].wait()
                    gone = gone_ref[...].astype(F32).T.astype(BF16)
                loads[t + 1].wait()
                for at in range(2):
                    table = held_ref[t, at * half : (at + 1) * half, :].astype(BF16)
                    lost = jnp.broadcast_to(gone[at * half : (at + 1) * half, t : t + 1], table.shape)
                    table_ref[t, :, at * emb : (at + 1) * emb] = jnp.where(
                        lost == jnp.zeros_like(lost), table, jnp.zeros_like(table)
                    )
            lines = slice(t * cap, (t + 1) * cap)
            picks, first = [], []
            for o in range(c * part, (c + 1) * part):
                row = jnp.broadcast_to(signed[lines, o : o + 1], (cap, emb))
                at = jnp.abs(row)
                picks.append(
                    jnp.concatenate([jnp.where(at == n, one, zero) for n in names], axis=1)
                )
                first.append(row > zero)
            both = dot(jnp.concatenate(picks, axis=0), table_ref[t]).astype(BF16)
            line = jnp.where(jnp.concatenate(first, axis=0), both[:, :emb], both[:, emb:])
            sent_ref[mine, lines, :] = line.reshape(part, cap, emb)
        store = pltpu.make_async_copy(sent_ref.at[mine], out_ref.at[mine], out_sem.at[c])
        store.start()
        stores.append(store)
    for store in stores:
        store.wait()


def wanted_kernel(arrived_ref, row_ref):
    width = arrived_ref.shape[1]
    tabs, _, slots = row_ref.shape
    cap = width // tabs
    own = own_lines(halves_of(arrived_ref[...], 128), slots)
    for t in range(tabs):
        for kind in range(2):
            row_ref[t, 8 * kind : 8 * kind + 8, :] = dot(
                of_table((8, 2 * width), 1, t, kind, width, cap), own, NT
            )


def sublanes(length, wide):
    column = iota((length, 128), 0).astype(F32).astype(BF16)
    return jnp.concatenate([column] * (wide // 128), axis=1)


def down(row, length):
    return jnp.concatenate([row] * (length // 8), axis=0).astype(BF16)


def pool_kernel(rows_ref, sample_ref, inv_ref, out_ref):
    groups, width, emb = rows_ref.shape
    tabs, toks, _ = inv_ref.shape
    cap = width // tabs
    slots = groups * cap
    one, zero = jnp.ones((toks, slots), BF16), jnp.zeros((toks, slots), BF16)
    samples = sublanes(toks, slots)
    for t in range(tabs):
        row = jnp.broadcast_to(sample_ref[t : t + 1, :] - 1.0, (16, slots)).astype(BF16)
        pick = jnp.where(jnp.concatenate([row] * (toks // 16), axis=0) == samples, one, zero)
        pooled = dot(pick, rows_ref[:, t * cap : (t + 1) * cap, :].reshape(slots, emb))
        feature = (pooled * inv_ref[t]).astype(BF16)
        for k in range(out_ref.shape[0]):
            out_ref[k, :, t * emb : (t + 1) * emb] = feature


def silu_slope(preact):
    sig = jax.nn.sigmoid(preact)
    return sig * (1.0 + preact * (1.0 - sig))


def dense_kernel(
    at_ref, feat_ref, own_ref, near_ref, far_ref, u0, u1, u2, u3, labels_ref,
    logits_ref, grad_ref, mine_ref, other_ref,
):
    parts, toks, feats = feat_ref.shape
    units = (u0, u1, u2, u3)
    me, core = at_ref[0], at_ref[1]
    order = [(2 * core + q) % parts for q in range(parts)]
    preacts, scores = [], []
    for k, u in enumerate(units):
        pre = jnp.zeros((toks, u.shape[1]), F32)
        for q, at in enumerate(order):
            if k == 0:
                w = own_ref[pl.ds(pl.multiple_of(at * feats, feats), feats), :]
            else:
                half = near_ref if q < parts // 2 else far_ref
                start = q % (parts // 2) * feats
                w = half[k - 1, start : start + feats, :]
            pre = pre + dot(feat_ref[at], w)
        hidden = jax.nn.silu(pre).astype(BF16).astype(F32)
        preacts.append(pre)
        scores.append(jnp.sum(hidden * u[...], axis=1, keepdims=True))
    logits = jnp.zeros((toks, 1), F32)
    for shard in range(parts):
        far = (me + parts - shard) % parts
        score = scores[0]
        for k in range(1, parts):
            score = jnp.where(far == k, scores[k], score)
        logits = logits + score
    dlogit = (jax.nn.sigmoid(logits) - labels_ref[...])[:, 0:1]
    logits_ref[...] = jnp.broadcast_to(logits, logits_ref.shape)
    grads = jnp.zeros((toks, feats), F32)
    for k, (u, pre) in enumerate(zip(units, preacts)):
        dhidden = (dlogit * u[...] * silu_slope(pre)).astype(BF16)
        if k == 0:
            half = dhidden.shape[1] // 2
            low, high = dhidden[:, :half], dhidden[:, half:]
            mine, other = jnp.where(core == 0, low, high), jnp.where(core == 0, high, low)
            for q in range(parts):
                lines = slice(q * feats, (q + 1) * feats)
                part = dot(
                    feat_ref[q],
                    jnp.concatenate([mine, other], axis=1),
                    (((0,), (0,)), ((), ())),
                ).astype(BF16)
                mine_ref[lines, :] = part[:, :half]
                other_ref[lines, :] = part[:, half:]
            w = own_ref[pl.ds(pl.multiple_of(me * feats, feats), feats), :]
        else:
            lines = pl.ds(pl.multiple_of(me % (parts // 2) * feats, feats), feats)
            w = jnp.where(
                me // (parts // 2) == core, near_ref[k - 1, lines, :], far_ref[k - 1, lines, :]
            )
        grads = grads + dot(dhidden, w, NT)
    grad_ref[...] = grads


def spread_kernel(grad_ref, inv_ref, pick_ref, out_ref):
    slots = pick_ref.shape[1]
    cap, emb = out_ref.shape[1:]
    grad = (inv_ref[0] * grad_ref[...]).astype(BF16)
    out_ref[...] = dot(pick_ref[0], grad).astype(BF16).reshape(slots // cap, cap, emb)


def update_kernel(grads_ref, wanted_ref, emb_ref, expired_ref, acc_ref, new_ref, new_acc_ref):
    groups, cap, emb = grads_ref.shape
    rows = emb_ref.shape[1]
    slots = groups * cap
    t = pl.program_id(0)
    grads = grads_ref[...].reshape(slots, emb)
    at = down(wanted_ref[0, 0:8, :], 16)
    low = down(wanted_ref[0, 8:16, :], 16)
    low = jnp.concatenate([low] * (emb // 16), axis=0)
    one, zero = jnp.ones((emb, slots), BF16), jnp.zeros((emb, slots), BF16)
    hot = jnp.where(low == sublanes(emb, slots), one, zero)
    gone = expired_ref[pl.ds(t, 1), :]
    fresh_acc = jnp.where(gone == 1, ACC_RESET, acc_ref[pl.ds(t, 1), :])
    kept = jnp.where(gone == 1, 0.0, 1.0)
    diag = iota((emb, emb), 0) == iota((emb, emb), 1)
    for j in range(0, rows, emb):
        here = jnp.concatenate([at == jnp.full_like(at, j // emb)] * (emb // 16), axis=0)
        summed = dot(jnp.where(here, hot, zero), grads)
        cols = slice(j, j + emb)
        old = jnp.sum(jnp.where(diag, fresh_acc[:, cols], 0.0), axis=1, keepdims=True)
        keep = jnp.sum(jnp.where(diag, kept[:, cols], 0.0), axis=1, keepdims=True)
        acc = old + jnp.sum(summed * summed, axis=1, keepdims=True) * (1.0 / emb)
        fresh = jnp.where(keep > 0.5, emb_ref[0, j : j + emb, :], 0.0)
        new_ref[0, j : j + emb, :] = fresh - LEARN_RATE * summed / jnp.sqrt(acc)
        line = jnp.sum(jnp.where(diag, acc, 0.0), axis=0, keepdims=True)
        for table in range(acc_ref.shape[0]):

            @pl.when(t == table)
            def _(table=table, cols=cols, line=line):
                new_acc_ref[table : table + 1, cols] = line


def shape(dims, dtype):
    return jax.ShapeDtypeStruct(dims, dtype)


def block(dims, index=None):
    if index is None:
        return pl.BlockSpec(dims, lambda *_: (0,) * len(dims))
    return pl.BlockSpec(dims, index)


def params(mib):
    return pltpu.CompilerParams(vmem_limit_bytes=mib << 20)


def cost(flops):
    return pl.CostEstimate(flops=flops, bytes_accessed=1 << 20, transcendentals=0)


def a2a(value, axis):
    return lax.all_to_all(value, axis, split_axis=0, concat_axis=0, tiled=True)


def from_everyone(value, axis):
    size = lax.axis_size(axis)
    return a2a(jnp.broadcast_to(value[None], (size, *value.shape)), axis)


def ring(value, axis, step):
    size = lax.axis_size(axis)
    return lax.ppermute(value, axis, [(i, (i + step) % size) for i in range(size)])


def shards(
    bag_lengths, owners, row_slots, admit_mask, expired, embeddings, accumulator,
    hidden_weight, output_weight, labels,
):
    groups = lax.axis_size(DP)
    parts = lax.axis_size("mp")
    tabs, toks, bag = row_slots.shape
    rows, emb = embeddings.shape[1:]
    cap = 2 * toks * bag // groups
    width = tabs * cap
    slots = groups * cap
    feats = tabs * emb
    core = lax.axis_index(NEAR).astype(I32)
    place = jnp.stack([lax.axis_index("mp").astype(I32), core])

    request, sample, inv = pl.pallas_call(
        slots_kernel,
        out_shape=(
            shape((groups, width), I32),
            shape((groups, width), F32),
            shape((tabs, toks, toks), F32),
        ),
        compiler_params=params(24),
        name="slots",
    )(
        *map(
            functools.partial(pltpu.with_memory_space_constraint, memory_space=pltpu.HBM),
            (
                bag_lengths,
                owners[..., 0].swapaxes(1, 2),
                row_slots.swapaxes(1, 2),
                admit_mask.swapaxes(1, 2),
            ),
        )
    )
    arrived = a2a(request, DP)
    lines, units_dev = hidden_weight.shape
    weight, _ = lax.optimization_barrier((hidden_weight, request))
    mine = lax.dynamic_slice(weight, (core * (lines // 2), 0), (lines // 2, units_dev))
    near_weights = jnp.stack([ring(mine, "mp", k) for k in range(1, parts)])
    far_weights = ring(near_weights, NEAR, 1)
    pick, sample_row = pl.pallas_call(
        samples_kernel,
        out_shape=(
            pltpu.HBM((tabs, slots, toks), BF16),
            shape((tabs, slots), F32),
        ),
        compiler_params=params(24),
        cost_estimate=cost(4 << 30),
        name="samples",
    )(sample)
    held = functools.partial(pltpu.with_memory_space_constraint, memory_space=pltpu.HBM)
    smem, vmem, hbm = (
        pl.BlockSpec(memory_space=space) for space in (pltpu.SMEM, pltpu.VMEM, pltpu.HBM)
    )
    dma = pltpu.SemaphoreType.DMA
    fetched = pl.pallas_call(
        fetch_kernel,
        in_specs=[vmem, hbm, hbm],
        out_specs=hbm,
        out_shape=pltpu.HBM((groups, width, emb), BF16),
        scratch_shapes=[
            pltpu.VMEM((tabs, rows), I32),
            pltpu.VMEM((tabs, rows, emb), F32),
            pltpu.VMEM((tabs, rows // 2, 2 * emb), BF16),
            pltpu.VMEM((groups, width, emb), BF16),
            dma((tabs + 1,)),
            dma((8,)),
        ],
        compiler_params=params(24),
        name="fetch",
    )(arrived, held(expired), held(embeddings))
    returned = a2a(fetched, DP)
    unit, later = lax.optimization_barrier((output_weight, arrived))
    unit = unit.reshape(1, -1)
    units = [unit] + [ring(unit, "mp", k) for k in range(1, parts)]
    wanted = pl.pallas_call(
        wanted_kernel,
        out_shape=pltpu.HBM((tabs, 16, slots), F32),
        compiler_params=params(24),
        cost_estimate=cost(4 << 30),
        name="wanted",
    )(later)
    features = pl.pallas_call(
        pool_kernel,
        out_shape=shape((parts, toks, feats), BF16),
        compiler_params=params(24),
        name="pool",
    )(returned, sample_row, inv)
    features, place, near_weights, far_weights, units = lax.optimization_barrier(
        (features, place, near_weights, far_weights, units)
    )
    portion = a2a(features, "mp")
    label_column = pl.pallas_call(
        labels_kernel,
        out_shape=shape((toks, toks), F32),
        compiler_params=params(4),
        name="labels",
    )(labels.reshape(1, toks))
    half = units_dev // 2
    logits, grad, mine, other = pl.pallas_call(
        dense_kernel,
        in_specs=[smem] + [vmem] * (parts + 5),
        out_shape=(
            shape((toks, toks), F32),
            shape((toks, feats), F32),
            shape((lines, half), BF16),
            shape((lines, half), BF16),
        ),
        compiler_params=params(24),
        name="dense",
    )(place, portion, held(hidden_weight), near_weights, far_weights, *units, label_column)
    joined = ring(other, NEAR, 1)
    share = lines // groups
    outgoing = pl.pallas_call(
        spread_kernel,
        grid=(tabs,),
        in_specs=[
            block((toks, emb), lambda t: (0, t)),
            block((1, toks, toks), lambda t: (t, 0, 0)),
            block((1, slots, toks), lambda t: (t, 0, 0)),
        ],
        out_specs=block((groups, cap, emb), lambda t: (0, t, 0)),
        out_shape=shape((groups, width + share, emb), BF16),
        compiler_params=params(24),
        cost_estimate=cost(4 << 30),
        name="spread",
    )(grad, inv, pick)
    pair = (mine.astype(F32) + joined.astype(F32)).astype(BF16)
    pair = pair.reshape(2, groups // 2, share, half).swapaxes(0, 1)
    outgoing = lax.dynamic_update_slice(
        outgoing, pair.reshape(groups, share, half), (0, width, 0)
    )
    gradients = a2a(outgoing, DP)
    shares = gradients[:, width:].reshape(groups // 2, 2, 2, share // 2, half)
    own = shares.astype(F32).sum(axis=0).astype(BF16).swapaxes(0, 1)
    near = from_everyone(own, FAR)
    near = near.transpose(0, 1, 3, 2, 4).reshape(lines // 2, units_dev)
    far = ring(near, NEAR, 1)
    weight_grad = jnp.concatenate(
        [jnp.where(core == 0, near, far), jnp.where(core == 0, far, near)]
    )
    new_rows, new_acc = pl.pallas_call(
        update_kernel,
        grid=(tabs,),
        in_specs=[
            block((groups, cap, emb), lambda t: (0, t, 0)),
            block((1, 16, slots), lambda t: (t, 0, 0)),
            block((1, rows, emb), lambda t: (t, 0, 0)),
            block((tabs, rows)),
            block((tabs, rows)),
        ],
        out_specs=(
            block((1, rows, emb), lambda t: (t, 0, 0)),
            block((tabs, rows)),
        ),
        out_shape=(shape(embeddings.shape, F32), shape(accumulator.shape, F32)),
        compiler_params=params(24),
        cost_estimate=cost(4 << 30),
        name="update",
    )(gradients, held(wanted), held(embeddings), expired, accumulator)
    return (new_rows, new_acc, weight_grad, logits[:, 0])


def solution(mesh):
    split = Mesh(mesh.devices.reshape(8, 8, 2, mesh.shape["mp"]), (*DP, "mp"))

    return jax.shard_map(
        shards,
        mesh=split,
        in_specs=(
            P("mp", DP),
            P("mp", DP, None, None),
            P("mp", DP, None),
            P("mp", DP, None),
            P("mp", DP),
            P("mp", DP, None),
            P("mp", DP),
            P(None, "mp"),
            P("mp"),
            P(DP),
        ),
        out_specs=(P("mp", DP, None), P("mp", DP), P(None, "mp"), P(DP)),
        check_vma=False,
    )
```

profile of v0, /device:TPU:1, one launch (start us, length us, event | category | flops | bytes accessed | tf_op | source)
XLA Modules:
  0.0 233.7 jit_solution(1948016066863518956)
XLA Ops:
  2.5 29.7 %all_to_all.31 = s32[128,1,64]{2,1,0:T(1,128)S(1)} all-to-all(s32[128,1,64]{2,1,0:T(1,128)S(1)} %bitcast.27), channel_id=1, replica_groups=mesh['dp_0'=8,'dp_1'=8,'dp_2'=2,'mp'=4] {'dp_0','dp_1','dp_2'}, dimensions={0} | all-to-all | bytes 65536 | tf_op jit(solution)/shard_map/all_to_all | solution.py:344
  32.2 4.0 %fetch.1 = bf16[128,64,128]{2,1,0:T(8,128)(2,1)} custom-call(s32[128,64]{1,0:T(8,128)S(1)} %bitcast.25, s32[4,512]{1,0:T(4,128)} %expired_ref.3, f32[4,512,128]{2,1,0:T(8,128)} %emb_ref.3), custom_call_target="tpu_custom_call" | custom-call | tf_op jit(solution)/shard_map/fetch/pallas_call | solution.py:413
  36.3 5.9 %all-to-all-start.1 = ((bf16[128,64,128]{2,1,0:T(8,128)(2,1)}), bf16[128,64,128]{2,1,0:T(8,128)(2,1)S(1)}, u32[]{:S(2)}, u32[]{:S(2)}) async-start(bf16[128,64,128]{2,1,0:T(8,128)(2,1)} %fetch.1), calls=%async_computation.1 | async-start | bytes 4194304 | tf_op jit(solution)/shard_map/all_to_all | solution.py:344
  42.2 4.4 %collective-permute-start.2 = (bf16[1024,256]{1,0:T(8,128)(2,1)S(1)}, bf16[1024,256]{1,0:T(8,128)(2,1)S(1)}, u32[]{:S(2)}, u32[]{:S(2)}) collective-permute-start(bf16[1024,256]{1,0:T(8,128)(2,1)S(1)} %constant_dynamic-slice_fusion), channel_id=1, source_target_pairs={{0,3},{1,0},{2,1},{3,2},{4,7},{5,4},{6,5},{7,6},{8,11},{9,8},{10,9... | collective-permute-start | bytes 1572872 | tf_op jit(solution)/shard_map/ppermute | solution.py:354
  46.6 2.4 %collective-permute-start.1 = (bf16[1024,256]{1,0:T(8,128)(2,1)S(1)}, bf16[1024,256]{1,0:T(8,128)(2,1)S(1)}, u32[]{:S(2)}, u32[]{:S(2)}) collective-permute-start(bf16[1024,256]{1,0:T(8,128)(2,1)S(1)} %constant_dynamic-slice_fusion), channel_id=1, source_target_pairs={{0,2},{1,3},{2,0},{3,1},{4,6},{5,7},{6,4},{7,5},{8,10},{9,11},{10,... | collective-permute-start | bytes 1572872 | tf_op jit(solution)/shard_map/ppermute | solution.py:354
  49.1 2.5 %collective-permute-start = (bf16[1024,256]{1,0:T(8,128)(2,1)S(1)}, bf16[1024,256]{1,0:T(8,128)(2,1)S(1)}, u32[]{:S(2)}, u32[]{:S(2)}) collective-permute-start(bf16[1024,256]{1,0:T(8,128)(2,1)S(1)} %constant_dynamic-slice_fusion), channel_id=1, source_target_pairs={{0,1},{1,2},{2,3},{3,0},{4,5},{5,6},{6,7},{7,4},{8,9},{9,10},{10,1... | collective-permute-start | bytes 1572872 | tf_op jit(solution)/shard_map/ppermute | solution.py:354
  51.6 6.1 %collective-permute-done.2 = bf16[1024,256]{1,0:T(8,128)(2,1)S(1)} collective-permute-done((bf16[1024,256]{1,0:T(8,128)(2,1)S(1)}, bf16[1024,256]{1,0:T(8,128)(2,1)S(1)}, u32[]{:S(2)}, u32[]{:S(2)}) %collective-permute-start.2) | collective-permute-done | bytes 524320 | tf_op jit(solution)/shard_map/ppermute | solution.py:354
  57.7 4.6 %collective-permute-done.1 = bf16[1024,256]{1,0:T(8,128)(2,1)S(1)} collective-permute-done((bf16[1024,256]{1,0:T(8,128)(2,1)S(1)}, bf16[1024,256]{1,0:T(8,128)(2,1)S(1)}, u32[]{:S(2)}, u32[]{:S(2)}) %collective-permute-start.1) | collective-permute-done | bytes 524320 | tf_op jit(solution)/shard_map/ppermute | solution.py:354
  62.3 12.8 %collective-permute-done = bf16[1024,256]{1,0:T(8,128)(2,1)S(1)} collective-permute-done((bf16[1024,256]{1,0:T(8,128)(2,1)S(1)}, bf16[1024,256]{1,0:T(8,128)(2,1)S(1)}, u32[]{:S(2)}, u32[]{:S(2)}) %collective-permute-start) | collective-permute-done | bytes 524320 | tf_op jit(solution)/shard_map/ppermute | solution.py:354
  76.5 2.4 %collective-permute-start.3 = (bf16[3,1024,256]{2,1,0:T(8,128)(2,1)}, bf16[3,1024,256]{2,1,0:T(8,128)(2,1)}, u32[]{:S(2)}, u32[]{:S(2)}) collective-permute-start(bf16[3,1024,256]{2,1,0:T(8,128)(2,1)} %pad_maximum_fusion.near_ref), channel_id=1, source_target_pairs={{0,4},{4,0},{1,5},{5,1},{2,6},{6,2},{3,7},{7,3},{8,12},{12,8},{9,1... | collective-permute-start | bytes 4718600 | tf_op jit(solution)/shard_map/ppermute | solution.py:354
  78.9 2.5 %samples.1 = (bf16[4,2048,128]{2,1,0:T(8,128)(2,1)}, f32[4,2048]{1,0:T(4,128)S(1)}) custom-call(f32[128,64]{1,0:T(8,128)S(1)} %get-tuple-element.27.sample_ref), custom_call_target="tpu_custom_call" | custom-call | flops 4294967296 | bytes 1048576 | tf_op jit(solution)/shard_map/samples/pallas_call | solution.py:398
  83.5 3.4 %collective-permute-start.5 = (f32[1,256]{1,0:T(1,128)S(1)}, f32[1,256]{1,0:T(1,128)S(1)}, u32[]{:S(2)}, u32[]{:S(2)}) collective-permute-start(f32[1,256]{1,0:T(1,128)S(1)} %bitcast.29), channel_id=1, source_target_pairs={{0,2},{1,3},{2,0},{3,1},{4,6},{5,7},{6,4},{7,5},{8,10},{9,11},{10,... | collective-permute-start | bytes 3080 | tf_op jit(solution)/shard_map/ppermute | solution.py:354
  86.9 3.1 %collective-permute-start.6 = (f32[1,256]{1,0:T(1,128)S(1)}, f32[1,256]{1,0:T(1,128)S(1)}, u32[]{:S(2)}, u32[]{:S(2)}) collective-permute-start(f32[1,256]{1,0:T(1,128)S(1)} %bitcast.30), channel_id=1, source_target_pairs={{0,3},{1,0},{2,1},{3,2},{4,7},{5,4},{6,5},{7,6},{8,11},{9,8},{10,9... | collective-permute-start | bytes 3080 | tf_op jit(solution)/shard_map/ppermute | solution.py:354
  90.1 3.5 %all-to-all-done.1.rows_ref = bf16[128,64,128]{2,1,0:T(8,128)(2,1)S(1)} async-done(((bf16[128,64,128]{2,1,0:T(8,128)(2,1)}), bf16[128,64,128]{2,1,0:T(8,128)(2,1)S(1)}, u32[]{:S(2)}, u32[]{:S(2)}) %all-to-all-start.1) | async-done | bytes 2097184 | tf_op jit(solution)/shard_map/all_to_all | solution.py:344
  95.1 4.0 %all-to-all-start.2 = ((bf16[4,128,512]{2,1,0:T(8,128)(2,1)}), bf16[4,128,512]{2,1,0:T(8,128)(2,1)S(1)}, u32[]{:S(2)}, u32[]{:S(2)}) async-start(bf16[4,128,512]{2,1,0:T(8,128)(2,1)} %pool.1), calls=%async_computation.2 | async-start | bytes 1048576 | tf_op jit(solution)/shard_map/all_to_all | solution.py:344
  99.2 6.9 %all-to-all-done.2.feat_ref = bf16[4,128,512]{2,1,0:T(8,128)(2,1)S(1)} async-done(((bf16[4,128,512]{2,1,0:T(8,128)(2,1)}), bf16[4,128,512]{2,1,0:T(8,128)(2,1)S(1)}, u32[]{:S(2)}, u32[]{:S(2)}) %all-to-all-start.2) | async-done | bytes 524320 | tf_op jit(solution)/shard_map/all_to_all | solution.py:344
  106.1 4.0 %dense.1 = (f32[128,128]{1,0:T(8,128)S(1)}, f32[128,512]{1,0:T(8,128)S(1)}, bf16[2048,128]{1,0:T(8,128)(2,1)S(1)}, bf16[2048,128]{1,0:T(8,128)(2,1)S(1)}) custom-call(s32[2]{0:T(128)S(1)} %pad_add_fusion.at_ref, bf16[4,128,512]{2,1,0:T(8,128)(2,1)S(1)} %all-to-all-done.2.feat_ref, bf16[2048,256]{1,0:T(8,128)(2,1)} %own_ref.1, ...), custom_call_target="tpu_custom_call" | custom-call | tf_op jit(solution)/shard_map/dense/pallas_call | solution.py:457
  110.1 5.5 %collective-permute-start.7 = (bf16[2048,128]{1,0:T(8,128)(2,1)S(1)}, bf16[2048,128]{1,0:T(8,128)(2,1)S(1)}, u32[]{:S(2)}, u32[]{:S(2)}) collective-permute-start(bf16[2048,128]{1,0:T(8,128)(2,1)S(1)} %get-tuple-element.43), channel_id=1, source_target_pairs={{0,4},{4,0},{1,5},{5,1},{2,6},{6,2},{3,7},{7,3},{8,12},{12,8},{9,1... | collective-permute-start | bytes 1572872 | tf_op jit(solution)/shard_map/ppermute | solution.py:354
  117.4 71.5 %all_to_all.32.grads_ref = bf16[128,80,128]{2,1,0:T(8,128)(2,1)S(1)} all-to-all(bf16[128,80,128]{2,1,0:T(8,128)(2,1)S(1)} %constant_dynamic-update-slice_fusion), channel_id=1, replica_groups=mesh['dp_0'=8,'dp_1'=8,'dp_2'=2,'mp'=4] {'dp_0','dp_1','dp_2'}, dimensions={0} | all-to-all | bytes 5242880 | tf_op jit(solution)/shard_map/all_to_all | solution.py:344
  189.9 9.2 %all-to-all-start.4 = ((bf16[64,2,2,8,128]{4,3,2,1,0:T(8,128)(2,1)}), bf16[64,2,2,8,128]{4,3,2,1,0:T(8,128)(2,1)S(1)}, u32[]{:S(2)}, u32[]{:S(2)}) async-start(bf16[64,2,2,8,128]{4,3,2,1,0:T(8,128)(2,1)} %broadcast_in_dim.2), calls=%async_computation.4 | async-start | bytes 1048576 | tf_op jit(solution)/shard_map/all_to_all | solution.py:344
  199.1 17.5 %all-to-all-done.4 = bf16[64,2,2,8,128]{4,3,2,1,0:T(8,128)(2,1)S(1)} async-done(((bf16[64,2,2,8,128]{4,3,2,1,0:T(8,128)(2,1)}), bf16[64,2,2,8,128]{4,3,2,1,0:T(8,128)(2,1)S(1)}, u32[]{:S(2)}, u32[]{:S(2)}) %all-to-all-start.4) | async-done | bytes 524320 | tf_op jit(solution)/shard_map/all_to_all | solution.py:344
  216.7 5.1 %collective-permute-start.8 = (bf16[1024,256]{1,0:T(8,128)(2,1)S(1)}, bf16[1024,256]{1,0:T(8,128)(2,1)S(1)}, u32[]{:S(2)}, u32[]{:S(2)}) collective-permute-start(bf16[1024,256]{1,0:T(8,128)(2,1)S(1)} %bitcast.33), channel_id=1, source_target_pairs={{0,4},{4,0},{1,5},{5,1},{2,6},{6,2},{3,7},{7,3},{8,12},{12,8},{9,1... | collective-permute-start | bytes 1572872 | tf_op jit(solution)/shard_map/ppermute | solution.py:354
  221.8 2.1 wanted.1.wanted_ref
  224.5 8.2 %update.1 = (f32[4,512,128]{2,1,0:T(8,128)}, f32[4,512]{1,0:T(4,128)}) custom-call(bf16[128,80,128]{2,1,0:T(8,128)(2,1)S(1)} %all_to_all.32.grads_ref, f32[4,16,2048]{2,1,0:T(8,128)} %wanted.1.wanted_ref, f32[4,512,128]{2,1,0:T(8,128)} %emb_ref.3, s32[4,512]{1,0:T(4,128)S(1)} %copy-done, f32[4,512]{1,0:T(4,128)S(1)} %copy-done.3), custom_call_target="tpu_custom_call" | custom-call | flops 4294967296 | bytes 1048576 | tf_op jit(solution)/shard_map/update/pallas_call | solution.py:499
  (36 shorter events, 11.5 us)
Async XLA Ops:
  36.2 5.9 %copy-start.5 = (bf16[2048,256]{1,0:T(8,128)(2,1)S(1)}, bf16[2048,256]{1,0:T(8,128)(2,1)}, u32[]{:S(2)}) copy-start(bf16[2048,256]{1,0:T(8,128)(2,1)} %own_ref.1) | copy-start | bytes 3145732
  36.3 57.3 %all-to-all-start.1 = ((bf16[128,64,128]{2,1,0:T(8,128)(2,1)}), bf16[128,64,128]{2,1,0:T(8,128)(2,1)S(1)}, u32[]{:S(2)}, u32[]{:S(2)}) async-start(bf16[128,64,128]{2,1,0:T(8,128)(2,1)} %fetch.1), calls=%async_computation.1 | async-start | bytes 4194304 | tf_op jit(solution)/shard_map/all_to_all | solution.py:344
  42.2 15.4 %collective-permute-start.2 = (bf16[1024,256]{1,0:T(8,128)(2,1)S(1)}, bf16[1024,256]{1,0:T(8,128)(2,1)S(1)}, u32[]{:S(2)}, u32[]{:S(2)}) collective-permute-start(bf16[1024,256]{1,0:T(8,128)(2,1)S(1)} %constant_dynamic-slice_fusion), channel_id=1, source_target_pairs={{0,3},{1,0},{2,1},{3,2},{4,7},{5,4},{6,5},{7,6},{8,11},{9,8},{10,9... | collective-permute-start | bytes 1572872 | tf_op jit(solution)/shard_map/ppermute | solution.py:354
  46.6 15.6 %collective-permute-start.1 = (bf16[1024,256]{1,0:T(8,128)(2,1)S(1)}, bf16[1024,256]{1,0:T(8,128)(2,1)S(1)}, u32[]{:S(2)}, u32[]{:S(2)}) collective-permute-start(bf16[1024,256]{1,0:T(8,128)(2,1)S(1)} %constant_dynamic-slice_fusion), channel_id=1, source_target_pairs={{0,2},{1,3},{2,0},{3,1},{4,6},{5,7},{6,4},{7,5},{8,10},{9,11},{10,... | collective-permute-start | bytes 1572872 | tf_op jit(solution)/shard_map/ppermute | solution.py:354
  49.1 26.0 %collective-permute-start = (bf16[1024,256]{1,0:T(8,128)(2,1)S(1)}, bf16[1024,256]{1,0:T(8,128)(2,1)S(1)}, u32[]{:S(2)}, u32[]{:S(2)}) collective-permute-start(bf16[1024,256]{1,0:T(8,128)(2,1)S(1)} %constant_dynamic-slice_fusion), channel_id=1, source_target_pairs={{0,1},{1,2},{2,3},{3,0},{4,5},{5,6},{6,7},{7,4},{8,9},{9,10},{10,1... | collective-permute-start | bytes 1572872 | tf_op jit(solution)/shard_map/ppermute | solution.py:354
  76.5 18.6 %collective-permute-start.3 = (bf16[3,1024,256]{2,1,0:T(8,128)(2,1)}, bf16[3,1024,256]{2,1,0:T(8,128)(2,1)}, u32[]{:S(2)}, u32[]{:S(2)}) collective-permute-start(bf16[3,1024,256]{2,1,0:T(8,128)(2,1)} %pad_maximum_fusion.near_ref), channel_id=1, source_target_pairs={{0,4},{4,0},{1,5},{5,1},{2,6},{6,2},{3,7},{7,3},{8,12},{12,8},{9,1... | collective-permute-start | bytes 4718600 | tf_op jit(solution)/shard_map/ppermute | solution.py:354
  78.9 2.5 %copy-start.1 = (f32[256]{0:T(256)S(1)}, f32[256]{0:T(256)}, u32[]{:S(2)}) copy-start(f32[256]{0:T(256)} %param.18) | copy-start | bytes 3076
  81.4 17.7 %copy-start.2 = (s32[128]{0:T(128)S(1)}, s32[128]{0:T(128)}, u32[]{:S(2)}) copy-start(s32[128]{0:T(128)} %param.19) | copy-start | bytes 1540
  81.4 13.6 %collective-permute-start.4 = (f32[1,256]{1,0:T(1,128)S(1)}, f32[1,256]{1,0:T(1,128)S(1)}, u32[]{:S(2)}, u32[]{:S(2)}) collective-permute-start(f32[1,256]{1,0:T(1,128)S(1)} %bitcast.28), channel_id=1, source_target_pairs={{0,1},{1,2},{2,3},{3,0},{4,5},{5,6},{6,7},{7,4},{8,9},{9,10},{10,1... | collective-permute-start | bytes 3080 | tf_op jit(solution)/shard_map/ppermute | solution.py:354
  83.5 11.6 %collective-permute-start.5 = (f32[1,256]{1,0:T(1,128)S(1)}, f32[1,256]{1,0:T(1,128)S(1)}, u32[]{:S(2)}, u32[]{:S(2)}) collective-permute-start(f32[1,256]{1,0:T(1,128)S(1)} %bitcast.29), channel_id=1, source_target_pairs={{0,2},{1,3},{2,0},{3,1},{4,6},{5,7},{6,4},{7,5},{8,10},{9,11},{10,... | collective-permute-start | bytes 3080 | tf_op jit(solution)/shard_map/ppermute | solution.py:354
  86.9 8.2 %collective-permute-start.6 = (f32[1,256]{1,0:T(1,128)S(1)}, f32[1,256]{1,0:T(1,128)S(1)}, u32[]{:S(2)}, u32[]{:S(2)}) collective-permute-start(f32[1,256]{1,0:T(1,128)S(1)} %bitcast.30), channel_id=1, source_target_pairs={{0,3},{1,0},{2,1},{3,2},{4,7},{5,4},{6,5},{7,6},{8,11},{9,8},{10,9... | collective-permute-start | bytes 3080 | tf_op jit(solution)/shard_map/ppermute | solution.py:354
  95.1 11.0 %all-to-all-start.2 = ((bf16[4,128,512]{2,1,0:T(8,128)(2,1)}), bf16[4,128,512]{2,1,0:T(8,128)(2,1)S(1)}, u32[]{:S(2)}, u32[]{:S(2)}) async-start(bf16[4,128,512]{2,1,0:T(8,128)(2,1)} %pool.1), calls=%async_computation.2 | async-start | bytes 1048576 | tf_op jit(solution)/shard_map/all_to_all | solution.py:344
  106.0 9.5 %copy-start.4 = (bf16[4,2048,128]{2,1,0:T(8,128)(2,1)S(1)}, bf16[4,2048,128]{2,1,0:T(8,128)(2,1)}, u32[]{:S(2)}) copy-start(bf16[4,2048,128]{2,1,0:T(8,128)(2,1)} %get-tuple-element.41.pick_ref) | copy-start | bytes 6291460
  110.1 7.0 %collective-permute-start.7 = (bf16[2048,128]{1,0:T(8,128)(2,1)S(1)}, bf16[2048,128]{1,0:T(8,128)(2,1)S(1)}, u32[]{:S(2)}, u32[]{:S(2)}) collective-permute-start(bf16[2048,128]{1,0:T(8,128)(2,1)S(1)} %get-tuple-element.43), channel_id=1, source_target_pairs={{0,4},{4,0},{1,5},{5,1},{2,6},{6,2},{3,7},{7,3},{8,12},{12,8},{9,1... | collective-permute-start | bytes 1572872 | tf_op jit(solution)/shard_map/ppermute | solution.py:354
  189.9 26.8 %all-to-all-start.4 = ((bf16[64,2,2,8,128]{4,3,2,1,0:T(8,128)(2,1)}), bf16[64,2,2,8,128]{4,3,2,1,0:T(8,128)(2,1)S(1)}, u32[]{:S(2)}, u32[]{:S(2)}) async-start(bf16[64,2,2,8,128]{4,3,2,1,0:T(8,128)(2,1)} %broadcast_in_dim.2), calls=%async_computation.4 | async-start | bytes 1048576 | tf_op jit(solution)/shard_map/all_to_all | solution.py:344
  216.6 7.8 %copy-start = (s32[4,512]{1,0:T(4,128)S(1)}, s32[4,512]{1,0:T(4,128)}, u32[]{:S(2)}) copy-start(s32[4,512]{1,0:T(4,128)} %expired_ref.3) | copy-start | bytes 24580
  216.7 7.8 %copy-start.3 = (f32[4,512]{1,0:T(4,128)S(1)}, f32[4,512]{1,0:T(4,128)}, u32[]{:S(2)}) copy-start(f32[4,512]{1,0:T(4,128)} %acc_ref.1) | copy-start | bytes 24580
  216.7 16.0 %collective-permute-start.8 = (bf16[1024,256]{1,0:T(8,128)(2,1)S(1)}, bf16[1024,256]{1,0:T(8,128)(2,1)S(1)}, u32[]{:S(2)}, u32[]{:S(2)}) collective-permute-start(bf16[1024,256]{1,0:T(8,128)(2,1)S(1)} %bitcast.33), channel_id=1, source_target_pairs={{0,4},{4,0},{1,5},{5,1},{2,6},{6,2},{3,7},{7,3},{8,12},{12,8},{9,1... | collective-permute-start | bytes 1572872 | tf_op jit(solution)/shard_map/ppermute | solution.py:354
where the time goes:
time: 235 us; the launch traced here: 234 us
  blocking collectives  101 us (43%)
  waiting for transfers between devices  51.5 us (22%)
  starting transfers between devices  50 us (21%)
  Pallas kernels  25.6 us (11%)
  other arithmetic  2.8 us (1%)
    all_to_all x2, blocking collectives, a2a(): return lax.all_to_all(value, axis, split_axis=0, concat_axis=0, tiled=True)  101 us
    ppermute x9, starting transfers between devices, ring(): lax.ppermute(value, axis, [(i, (i + step) % size) for i in range(size)])  30.8 us
    all_to_all x3, waiting for transfers between devices, a2a(): return lax.all_to_all(value, axis, split_axis=0, concat_axis=0, tiled=True)  27.8 us
    ppermute x9, waiting for transfers between devices, ring(): lax.ppermute(value, axis, [(i, (i + step) % size) for i in range(size)])  23.7 us
    all_to_all x3, starting transfers between devices, a2a(): return lax.all_to_all(value, axis, split_axis=0, concat_axis=0, tiled=True)  19.2 us
    pallas_call x1, Pallas kernels, shards(): pl.pallas_call(update_kernel, grid=(tabs,), in_specs=[block((groups, cap,...  8.17 us
  transfers between devices with their start and end apart: 12, of which 7 were waited for; matrix products, arithmetic and copies ran while one was open for 1% of the time, Pallas kernels for 7%

commit v1 on v0

--- a/solution.py
+++ b/solution.py
@@ -291,23 +291,29 @@
 
 
 def update_kernel(grads_ref, wanted_ref, emb_ref, expired_ref, acc_ref, new_ref, new_acc_ref):
-    groups, cap, emb = grads_ref.shape
-    rows = emb_ref.shape[1]
-    slots = groups * cap
+    groups, _, emb = grads_ref.shape
+    _, rows = expired_ref.shape
+    slots = wanted_ref.shape[2]
+    cap = slots // groups
     t = pl.program_id(0)
-    grads = grads_ref[...].reshape(slots, emb)
+    lines = pl.ds(pl.multiple_of(t * cap, cap), cap)
+    grads = grads_ref[:, lines, :].reshape(slots, emb)
     at = down(wanted_ref[0, 0:8, :], 16)
     low = down(wanted_ref[0, 8:16, :], 16)
     low = jnp.concatenate([low] * (emb // 16), axis=0)
     one, zero = jnp.ones((emb, slots), BF16), jnp.zeros((emb, slots), BF16)
     hot = jnp.where(low == sublanes(emb, slots), one, zero)
+    picks = []
+    for j in range(rows // emb):
+        here = jnp.concatenate([at == jnp.full_like(at, j)] * (emb // 16), axis=0)
+        picks.append(jnp.where(here, hot, zero))
+    sums = dot(jnp.concatenate(picks, axis=0), grads)
     gone = expired_ref[pl.ds(t, 1), :]
     fresh_acc = jnp.where(gone == 1, ACC_RESET, acc_ref[pl.ds(t, 1), :])
     kept = jnp.where(gone == 1, 0.0, 1.0)
     diag = iota((emb, emb), 0) == iota((emb, emb), 1)
     for j in range(0, rows, emb):
-        here = jnp.concatenate([at == jnp.full_like(at, j // emb)] * (emb // 16), axis=0)
-        summed = dot(jnp.where(here, hot, zero), grads)
+        summed = sums[j : j + emb]
         cols = slice(j, j + emb)
         old = jnp.sum(jnp.where(diag, fresh_acc[:, cols], 0.0), axis=1, keepdims=True)
         keep = jnp.sum(jnp.where(diag, kept[:, cols], 0.0), axis=1, keepdims=True)
@@ -500,7 +506,7 @@
         update_kernel,
         grid=(tabs,),
         in_specs=[
-            block((groups, cap, emb), lambda t: (0, t, 0)),
+            vmem,
             block((1, 16, slots), lambda t: (t, 0, 0)),
             block((1, rows, emb), lambda t: (t, 0, 0)),
             block((tabs, rows)),

time: 235 us -> 233 us (level)
  transfers between devices with their start and end apart: 12 -> 12, of which waited for: 7 -> 7; matrix products, arithmetic and copies ran while one was open for 1% -> 1% of each run, Pallas kernels for 7% -> 6%
where the time goes in v1:
time: 233 us; the launch traced here: 232 us
  blocking collectives  101 us (43%)
  waiting for transfers between devices  51.5 us (22%)
  starting transfers between devices  50 us (21%)
  Pallas kernels  23.7 us (10%)
  other arithmetic  2.8 us (1%)
    all_to_all x2, blocking collectives, a2a(): return lax.all_to_all(value, axis, split_axis=0, concat_axis=0, tiled=True)  101 us
    ppermute x9, starting transfers between devices, ring(): lax.ppermute(value, axis, [(i, (i + step) % size) for i in range(size)])  30.8 us
    all_to_all x3, waiting for transfers between devices, a2a(): return lax.all_to_all(value, axis, split_axis=0, concat_axis=0, tiled=True)  27.8 us
    ppermute x9, waiting for transfers between devices, ring(): lax.ppermute(value, axis, [(i, (i + step) % size) for i in range(size)])  23.7 us
    all_to_all x3, starting transfers between devices, a2a(): return lax.all_to_all(value, axis, split_axis=0, concat_axis=0, tiled=True)  19.2 us
    pallas_call x1, Pallas kernels, shards(): pl.pallas_call(update_kernel, grid=(tabs,), in_specs=[vmem, block((1, 16,...  6.3 us
  transfers between devices with their start and end apart: 12, of which 7 were waited for; matrix products, arithmetic and copies ran while one was open for 1% of the time, Pallas kernels for 6%

profile of v1, /device:TPU:1, one launch (start us, length us, event | category | flops | bytes accessed | tf_op | source)
XLA Modules:
  0.0 231.9 jit_solution(5748193328498207157)
XLA Ops:
  2.5 29.7 %all_to_all.31 = s32[128,1,64]{2,1,0:T(1,128)S(1)} all-to-all(s32[128,1,64]{2,1,0:T(1,128)S(1)} %bitcast.27), channel_id=1, replica_groups=mesh['dp_0'=8,'dp_1'=8,'dp_2'=2,'mp'=4] {'dp_0','dp_1','dp_2'}, dimensions={0} | all-to-all | bytes 65536 | tf_op jit(solution)/shard_map/all_to_all | solution.py:350
  32.2 4.0 %fetch.1 = bf16[128,64,128]{2,1,0:T(8,128)(2,1)} custom-call(s32[128,64]{1,0:T(8,128)S(1)} %bitcast.25, s32[4,512]{1,0:T(4,128)} %expired_ref.3, f32[4,512,128]{2,1,0:T(8,128)} %emb_ref.3), custom_call_target="tpu_custom_call" | custom-call | tf_op jit(solution)/shard_map/fetch/pallas_call | solution.py:419
  36.3 5.9 %all-to-all-start.1 = ((bf16[128,64,128]{2,1,0:T(8,128)(2,1)}), bf16[128,64,128]{2,1,0:T(8,128)(2,1)S(1)}, u32[]{:S(2)}, u32[]{:S(2)}) async-start(bf16[128,64,128]{2,1,0:T(8,128)(2,1)} %fetch.1), calls=%async_computation.1 | async-start | bytes 4194304 | tf_op jit(solution)/shard_map/all_to_all | solution.py:350
  42.2 4.4 %collective-permute-start.2 = (bf16[1024,256]{1,0:T(8,128)(2,1)S(1)}, bf16[1024,256]{1,0:T(8,128)(2,1)S(1)}, u32[]{:S(2)}, u32[]{:S(2)}) collective-permute-start(bf16[1024,256]{1,0:T(8,128)(2,1)S(1)} %constant_dynamic-slice_fusion), channel_id=1, source_target_pairs={{0,3},{1,0},{2,1},{3,2},{4,7},{5,4},{6,5},{7,6},{8,11},{9,8},{10,9... | collective-permute-start | bytes 1572872 | tf_op jit(solution)/shard_map/ppermute | solution.py:360
  46.6 2.4 %collective-permute-start.1 = (bf16[1024,256]{1,0:T(8,128)(2,1)S(1)}, bf16[1024,256]{1,0:T(8,128)(2,1)S(1)}, u32[]{:S(2)}, u32[]{:S(2)}) collective-permute-start(bf16[1024,256]{1,0:T(8,128)(2,1)S(1)} %constant_dynamic-slice_fusion), channel_id=1, source_target_pairs={{0,2},{1,3},{2,0},{3,1},{4,6},{5,7},{6,4},{7,5},{8,10},{9,11},{10,... | collective-permute-start | bytes 1572872 | tf_op jit(solution)/shard_map/ppermute | solution.py:360
  49.1 2.5 %collective-permute-start = (bf16[1024,256]{1,0:T(8,128)(2,1)S(1)}, bf16[1024,256]{1,0:T(8,128)(2,1)S(1)}, u32[]{:S(2)}, u32[]{:S(2)}) collective-permute-start(bf16[1024,256]{1,0:T(8,128)(2,1)S(1)} %constant_dynamic-slice_fusion), channel_id=1, source_target_pairs={{0,1},{1,2},{2,3},{3,0},{4,5},{5,6},{6,7},{7,4},{8,9},{9,10},{10,1... | collective-permute-start | bytes 1572872 | tf_op jit(solution)/shard_map/ppermute | solution.py:360
  51.6 6.1 %collective-permute-done.2 = bf16[1024,256]{1,0:T(8,128)(2,1)S(1)} collective-permute-done((bf16[1024,256]{1,0:T(8,128)(2,1)S(1)}, bf16[1024,256]{1,0:T(8,128)(2,1)S(1)}, u32[]{:S(2)}, u32[]{:S(2)}) %collective-permute-start.2) | collective-permute-done | bytes 524320 | tf_op jit(solution)/shard_map/ppermute | solution.py:360
  57.7 4.6 %collective-permute-done.1 = bf16[1024,256]{1,0:T(8,128)(2,1)S(1)} collective-permute-done((bf16[1024,256]{1,0:T(8,128)(2,1)S(1)}, bf16[1024,256]{1,0:T(8,128)(2,1)S(1)}, u32[]{:S(2)}, u32[]{:S(2)}) %collective-permute-start.1) | collective-permute-done | bytes 524320 | tf_op jit(solution)/shard_map/ppermute | solution.py:360
  62.3 12.8 %collective-permute-done = bf16[1024,256]{1,0:T(8,128)(2,1)S(1)} collective-permute-done((bf16[1024,256]{1,0:T(8,128)(2,1)S(1)}, bf16[1024,256]{1,0:T(8,128)(2,1)S(1)}, u32[]{:S(2)}, u32[]{:S(2)}) %collective-permute-start) | collective-permute-done | bytes 524320 | tf_op jit(solution)/shard_map/ppermute | solution.py:360
  76.5 2.4 %collective-permute-start.3 = (bf16[3,1024,256]{2,1,0:T(8,128)(2,1)}, bf16[3,1024,256]{2,1,0:T(8,128)(2,1)}, u32[]{:S(2)}, u32[]{:S(2)}) collective-permute-start(bf16[3,1024,256]{2,1,0:T(8,128)(2,1)} %pad_maximum_fusion.near_ref), channel_id=1, source_target_pairs={{0,4},{4,0},{1,5},{5,1},{2,6},{6,2},{3,7},{7,3},{8,12},{12,8},{9,1... | collective-permute-start | bytes 4718600 | tf_op jit(solution)/shard_map/ppermute | solution.py:360
  78.9 2.5 %samples.1 = (bf16[4,2048,128]{2,1,0:T(8,128)(2,1)}, f32[4,2048]{1,0:T(4,128)S(1)}) custom-call(f32[128,64]{1,0:T(8,128)S(1)} %get-tuple-element.27.sample_ref), custom_call_target="tpu_custom_call" | custom-call | flops 4294967296 | bytes 1048576 | tf_op jit(solution)/shard_map/samples/pallas_call | solution.py:404
  83.5 3.4 %collective-permute-start.5 = (f32[1,256]{1,0:T(1,128)S(1)}, f32[1,256]{1,0:T(1,128)S(1)}, u32[]{:S(2)}, u32[]{:S(2)}) collective-permute-start(f32[1,256]{1,0:T(1,128)S(1)} %bitcast.29), channel_id=1, source_target_pairs={{0,2},{1,3},{2,0},{3,1},{4,6},{5,7},{6,4},{7,5},{8,10},{9,11},{10,... | collective-permute-start | bytes 3080 | tf_op jit(solution)/shard_map/ppermute | solution.py:360
  86.9 3.1 %collective-permute-start.6 = (f32[1,256]{1,0:T(1,128)S(1)}, f32[1,256]{1,0:T(1,128)S(1)}, u32[]{:S(2)}, u32[]{:S(2)}) collective-permute-start(f32[1,256]{1,0:T(1,128)S(1)} %bitcast.30), channel_id=1, source_target_pairs={{0,3},{1,0},{2,1},{3,2},{4,7},{5,4},{6,5},{7,6},{8,11},{9,8},{10,9... | collective-permute-start | bytes 3080 | tf_op jit(solution)/shard_map/ppermute | solution.py:360
  90.1 3.5 %all-to-all-done.1.rows_ref = bf16[128,64,128]{2,1,0:T(8,128)(2,1)S(1)} async-done(((bf16[128,64,128]{2,1,0:T(8,128)(2,1)}), bf16[128,64,128]{2,1,0:T(8,128)(2,1)S(1)}, u32[]{:S(2)}, u32[]{:S(2)}) %all-to-all-start.1) | async-done | bytes 2097184 | tf_op jit(solution)/shard_map/all_to_all | solution.py:350
  95.1 4.0 %all-to-all-start.2 = ((bf16[4,128,512]{2,1,0:T(8,128)(2,1)}), bf16[4,128,512]{2,1,0:T(8,128)(2,1)S(1)}, u32[]{:S(2)}, u32[]{:S(2)}) async-start(bf16[4,128,512]{2,1,0:T(8,128)(2,1)} %pool.1), calls=%async_computation.2 | async-start | bytes 1048576 | tf_op jit(solution)/shard_map/all_to_all | solution.py:350
  99.2 6.9 %all-to-all-done.2.feat_ref = bf16[4,128,512]{2,1,0:T(8,128)(2,1)S(1)} async-done(((bf16[4,128,512]{2,1,0:T(8,128)(2,1)}), bf16[4,128,512]{2,1,0:T(8,128)(2,1)S(1)}, u32[]{:S(2)}, u32[]{:S(2)}) %all-to-all-start.2) | async-done | bytes 524320 | tf_op jit(solution)/shard_map/all_to_all | solution.py:350
  106.1 4.0 %dense.1 = (f32[128,128]{1,0:T(8,128)S(1)}, f32[128,512]{1,0:T(8,128)S(1)}, bf16[2048,128]{1,0:T(8,128)(2,1)S(1)}, bf16[2048,128]{1,0:T(8,128)(2,1)S(1)}) custom-call(s32[2]{0:T(128)S(1)} %pad_add_fusion.at_ref, bf16[4,128,512]{2,1,0:T(8,128)(2,1)S(1)} %all-to-all-done.2.feat_ref, bf16[2048,256]{1,0:T(8,128)(2,1)} %own_ref.1, ...), custom_call_target="tpu_custom_call" | custom-call | tf_op jit(solution)/shard_map/dense/pallas_call | solution.py:463
  110.1 5.5 %collective-permute-start.7 = (bf16[2048,128]{1,0:T(8,128)(2,1)S(1)}, bf16[2048,128]{1,0:T(8,128)(2,1)S(1)}, u32[]{:S(2)}, u32[]{:S(2)}) collective-permute-start(bf16[2048,128]{1,0:T(8,128)(2,1)S(1)} %get-tuple-element.43), channel_id=1, source_target_pairs={{0,4},{4,0},{1,5},{5,1},{2,6},{6,2},{3,7},{7,3},{8,12},{12,8},{9,1... | collective-permute-start | bytes 1572872 | tf_op jit(solution)/shard_map/ppermute | solution.py:360
  117.4 71.5 %all_to_all.32.grads_ref = bf16[128,80,128]{2,1,0:T(8,128)(2,1)S(1)} all-to-all(bf16[128,80,128]{2,1,0:T(8,128)(2,1)S(1)} %constant_dynamic-update-slice_fusion), channel_id=1, replica_groups=mesh['dp_0'=8,'dp_1'=8,'dp_2'=2,'mp'=4] {'dp_0','dp_1','dp_2'}, dimensions={0} | all-to-all | bytes 5242880 | tf_op jit(solution)/shard_map/all_to_all | solution.py:350
  189.9 9.2 %all-to-all-start.4 = ((bf16[64,2,2,8,128]{4,3,2,1,0:T(8,128)(2,1)}), bf16[64,2,2,8,128]{4,3,2,1,0:T(8,128)(2,1)S(1)}, u32[]{:S(2)}, u32[]{:S(2)}) async-start(bf16[64,2,2,8,128]{4,3,2,1,0:T(8,128)(2,1)} %broadcast_in_dim.2), calls=%async_computation.4 | async-start | bytes 1048576 | tf_op jit(solution)/shard_map/all_to_all | solution.py:350
  199.1 17.5 %all-to-all-done.4 = bf16[64,2,2,8,128]{4,3,2,1,0:T(8,128)(2,1)S(1)} async-done(((bf16[64,2,2,8,128]{4,3,2,1,0:T(8,128)(2,1)}), bf16[64,2,2,8,128]{4,3,2,1,0:T(8,128)(2,1)S(1)}, u32[]{:S(2)}, u32[]{:S(2)}) %all-to-all-start.4) | async-done | bytes 524320 | tf_op jit(solution)/shard_map/all_to_all | solution.py:350
  216.7 5.1 %collective-permute-start.8 = (bf16[1024,256]{1,0:T(8,128)(2,1)S(1)}, bf16[1024,256]{1,0:T(8,128)(2,1)S(1)}, u32[]{:S(2)}, u32[]{:S(2)}) collective-permute-start(bf16[1024,256]{1,0:T(8,128)(2,1)S(1)} %bitcast.33), channel_id=1, source_target_pairs={{0,4},{4,0},{1,5},{5,1},{2,6},{6,2},{3,7},{7,3},{8,12},{12,8},{9,1... | collective-permute-start | bytes 1572872 | tf_op jit(solution)/shard_map/ppermute | solution.py:360
  221.8 2.1 wanted.1.wanted_ref
  224.5 6.3 %update.1 = (f32[4,512,128]{2,1,0:T(8,128)}, f32[4,512]{1,0:T(4,128)}) custom-call(bf16[128,80,128]{2,1,0:T(8,128)(2,1)S(1)} %all_to_all.32.grads_ref, f32[4,16,2048]{2,1,0:T(8,128)} %wanted.1.wanted_ref, f32[4,512,128]{2,1,0:T(8,128)} %emb_ref.3, s32[4,512]{1,0:T(4,128)S(1)} %copy-done, f32[4,512]{1,0:T(4,128)S(1)} %copy-done.3), custom_call_target="tpu_custom_call" | custom-call | flops 4294967296 | bytes 1048576 | tf_op jit(solution)/shard_map/update/pallas_call | solution.py:505
  (36 shorter events, 11.5 us)
Async XLA Ops:
  36.2 5.9 %copy-start.5 = (bf16[2048,256]{1,0:T(8,128)(2,1)S(1)}, bf16[2048,256]{1,0:T(8,128)(2,1)}, u32[]{:S(2)}) copy-start(bf16[2048,256]{1,0:T(8,128)(2,1)} %own_ref.1) | copy-start | bytes 3145732
  36.3 57.3 %all-to-all-start.1 = ((bf16[128,64,128]{2,1,0:T(8,128)(2,1)}), bf16[128,64,128]{2,1,0:T(8,128)(2,1)S(1)}, u32[]{:S(2)}, u32[]{:S(2)}) async-start(bf16[128,64,128]{2,1,0:T(8,128)(2,1)} %fetch.1), calls=%async_computation.1 | async-start | bytes 4194304 | tf_op jit(solution)/shard_map/all_to_all | solution.py:350
  42.2 15.4 %collective-permute-start.2 = (bf16[1024,256]{1,0:T(8,128)(2,1)S(1)}, bf16[1024,256]{1,0:T(8,128)(2,1)S(1)}, u32[]{:S(2)}, u32[]{:S(2)}) collective-permute-start(bf16[1024,256]{1,0:T(8,128)(2,1)S(1)} %constant_dynamic-slice_fusion), channel_id=1, source_target_pairs={{0,3},{1,0},{2,1},{3,2},{4,7},{5,4},{6,5},{7,6},{8,11},{9,8},{10,9... | collective-permute-start | bytes 1572872 | tf_op jit(solution)/shard_map/ppermute | solution.py:360
  46.6 15.6 %collective-permute-start.1 = (bf16[1024,256]{1,0:T(8,128)(2,1)S(1)}, bf16[1024,256]{1,0:T(8,128)(2,1)S(1)}, u32[]{:S(2)}, u32[]{:S(2)}) collective-permute-start(bf16[1024,256]{1,0:T(8,128)(2,1)S(1)} %constant_dynamic-slice_fusion), channel_id=1, source_target_pairs={{0,2},{1,3},{2,0},{3,1},{4,6},{5,7},{6,4},{7,5},{8,10},{9,11},{10,... | collective-permute-start | bytes 1572872 | tf_op jit(solution)/shard_map/ppermute | solution.py:360
  49.1 26.0 %collective-permute-start = (bf16[1024,256]{1,0:T(8,128)(2,1)S(1)}, bf16[1024,256]{1,0:T(8,128)(2,1)S(1)}, u32[]{:S(2)}, u32[]{:S(2)}) collective-permute-start(bf16[1024,256]{1,0:T(8,128)(2,1)S(1)} %constant_dynamic-slice_fusion), channel_id=1, source_target_pairs={{0,1},{1,2},{2,3},{3,0},{4,5},{5,6},{6,7},{7,4},{8,9},{9,10},{10,1... | collective-permute-start | bytes 1572872 | tf_op jit(solution)/shard_map/ppermute | solution.py:360
  76.5 18.6 %collective-permute-start.3 = (bf16[3,1024,256]{2,1,0:T(8,128)(2,1)}, bf16[3,1024,256]{2,1,0:T(8,128)(2,1)}, u32[]{:S(2)}, u32[]{:S(2)}) collective-permute-start(bf16[3,1024,256]{2,1,0:T(8,128)(2,1)} %pad_maximum_fusion.near_ref), channel_id=1, source_target_pairs={{0,4},{4,0},{1,5},{5,1},{2,6},{6,2},{3,7},{7,3},{8,12},{12,8},{9,1... | collective-permute-start | bytes 4718600 | tf_op jit(solution)/shard_map/ppermute | solution.py:360
  78.9 2.5 %copy-start.1 = (f32[256]{0:T(256)S(1)}, f32[256]{0:T(256)}, u32[]{:S(2)}) copy-start(f32[256]{0:T(256)} %param.18) | copy-start | bytes 3076
  81.4 17.7 %copy-start.2 = (s32[128]{0:T(128)S(1)}, s32[128]{0:T(128)}, u32[]{:S(2)}) copy-start(s32[128]{0:T(128)} %param.19) | copy-start | bytes 1540
  81.4 13.6 %collective-permute-start.4 = (f32[1,256]{1,0:T(1,128)S(1)}, f32[1,256]{1,0:T(1,128)S(1)}, u32[]{:S(2)}, u32[]{:S(2)}) collective-permute-start(f32[1,256]{1,0:T(1,128)S(1)} %bitcast.28), channel_id=1, source_target_pairs={{0,1},{1,2},{2,3},{3,0},{4,5},{5,6},{6,7},{7,4},{8,9},{9,10},{10,1... | collective-permute-start | bytes 3080 | tf_op jit(solution)/shard_map/ppermute | solution.py:360
  83.5 11.6 %collective-permute-start.5 = (f32[1,256]{1,0:T(1,128)S(1)}, f32[1,256]{1,0:T(1,128)S(1)}, u32[]{:S(2)}, u32[]{:S(2)}) collective-permute-start(f32[1,256]{1,0:T(1,128)S(1)} %bitcast.29), channel_id=1, source_target_pairs={{0,2},{1,3},{2,0},{3,1},{4,6},{5,7},{6,4},{7,5},{8,10},{9,11},{10,... | collective-permute-start | bytes 3080 | tf_op jit(solution)/shard_map/ppermute | solution.py:360
  86.9 8.2 %collective-permute-start.6 = (f32[1,256]{1,0:T(1,128)S(1)}, f32[1,256]{1,0:T(1,128)S(1)}, u32[]{:S(2)}, u32[]{:S(2)}) collective-permute-start(f32[1,256]{1,0:T(1,128)S(1)} %bitcast.30), channel_id=1, source_target_pairs={{0,3},{1,0},{2,1},{3,2},{4,7},{5,4},{6,5},{7,6},{8,11},{9,8},{10,9... | collective-permute-start | bytes 3080 | tf_op jit(solution)/shard_map/ppermute | solution.py:360
  95.1 11.0 %all-to-all-start.2 = ((bf16[4,128,512]{2,1,0:T(8,128)(2,1)}), bf16[4,128,512]{2,1,0:T(8,128)(2,1)S(1)}, u32[]{:S(2)}, u32[]{:S(2)}) async-start(bf16[4,128,512]{2,1,0:T(8,128)(2,1)} %pool.1), calls=%async_computation.2 | async-start | bytes 1048576 | tf_op jit(solution)/shard_map/all_to_all | solution.py:350
  106.0 9.5 %copy-start.4 = (bf16[4,2048,128]{2,1,0:T(8,128)(2,1)S(1)}, bf16[4,2048,128]{2,1,0:T(8,128)(2,1)}, u32[]{:S(2)}) copy-start(bf16[4,2048,128]{2,1,0:T(8,128)(2,1)} %get-tuple-element.41.pick_ref) | copy-start | bytes 6291460
  110.1 7.0 %collective-permute-start.7 = (bf16[2048,128]{1,0:T(8,128)(2,1)S(1)}, bf16[2048,128]{1,0:T(8,128)(2,1)S(1)}, u32[]{:S(2)}, u32[]{:S(2)}) collective-permute-start(bf16[2048,128]{1,0:T(8,128)(2,1)S(1)} %get-tuple-element.43), channel_id=1, source_target_pairs={{0,4},{4,0},{1,5},{5,1},{2,6},{6,2},{3,7},{7,3},{8,12},{12,8},{9,1... | collective-permute-start | bytes 1572872 | tf_op jit(solution)/shard_map/ppermute | solution.py:360
  189.9 26.8 %all-to-all-start.4 = ((bf16[64,2,2,8,128]{4,3,2,1,0:T(8,128)(2,1)}), bf16[64,2,2,8,128]{4,3,2,1,0:T(8,128)(2,1)S(1)}, u32[]{:S(2)}, u32[]{:S(2)}) async-start(bf16[64,2,2,8,128]{4,3,2,1,0:T(8,128)(2,1)} %broadcast_in_dim.2), calls=%async_computation.4 | async-start | bytes 1048576 | tf_op jit(solution)/shard_map/all_to_all | solution.py:350
  216.6 7.8 %copy-start = (s32[4,512]{1,0:T(4,128)S(1)}, s32[4,512]{1,0:T(4,128)}, u32[]{:S(2)}) copy-start(s32[4,512]{1,0:T(4,128)} %expired_ref.3) | copy-start | bytes 24580
  216.7 7.8 %copy-start.3 = (f32[4,512]{1,0:T(4,128)S(1)}, f32[4,512]{1,0:T(4,128)}, u32[]{:S(2)}) copy-start(f32[4,512]{1,0:T(4,128)} %acc_ref.1) | copy-start | bytes 24580
  216.7 14.1 %collective-permute-start.8 = (bf16[1024,256]{1,0:T(8,128)(2,1)S(1)}, bf16[1024,256]{1,0:T(8,128)(2,1)S(1)}, u32[]{:S(2)}, u32[]{:S(2)}) collective-permute-start(bf16[1024,256]{1,0:T(8,128)(2,1)S(1)} %bitcast.33), channel_id=1, source_target_pairs={{0,4},{4,0},{1,5},{5,1},{2,6},{6,2},{3,7},{7,3},{8,12},{12,8},{9,1... | collective-permute-start | bytes 1572872 | tf_op jit(solution)/shard_map/ppermute | solution.py:360
